TPU v7x, 32 devices: a whole 2x2x4 slice. The times are simulated.
32 devices in a mesh: dp: 8 (over y, x, core), vocab: 4 (over z).
Axes of the slice: x: 2, y: 2, z: 4, core: 2. Of those that a mesh axis runs over, the one named last changes fastest.
Arguments:
- hidden: bfloat16 [64, 4096], P('dp'), may hold values from -16 to 16
- embed_grad: bfloat16 [64, 4096], P('dp'), may hold values from -3 to 3
- token_ids: int32 [64], P('dp'), may hold values from 0 to 32767
- loss_weight: float32 [64], P('dp'), may hold values from 16 to 256
- teacher_logits: bfloat16 [64, 32768], P('dp', 'vocab'), may hold values from -24 to 256
- head: bfloat16 [4096, 32768], P('dp', 'vocab'), may hold values from -1 to 1
Outputs:
- grad_hidden: bfloat16 [64, 4096], P('dp', 'vocab')
- head_grad: float32 [4096, 32768], P('dp', 'vocab')
Inputs may be any that keep to these rules, and one draw needn't show every extreme that they name: `token_ids`: token ids of the vocabulary window.
All inputs are finite; a program needn't handle non-finite values.
Results may differ from a plain program's by a relative error of at most 0.0022.
The roundings to bfloat16 on the way count: a program that leaves them out, or rounds other values in their place, can miss the bound.
Values may be sent and summed in bfloat16 or wider, within the bound.
A program may use at most 128 MiB of HBM per device.

v0:
```python
import jax
import jax.numpy as jnp
from jax import lax
from jax.sharding import PartitionSpec as P


def combined_all(part, axis, combine):
    gathered = jax.tree.map(lambda a: lax.all_gather(a, axis), part)

    def take(source):
        return jax.tree.map(lambda a: lax.dynamic_index_in_dim(a, source, 0, False), gathered)

    return lax.fori_loop(
        1, lax.axis_size(axis), lambda source, state: combine(state, take(source)), take(0)
    )


def contract_rows(left, right):
    return lax.dot_general(
        left, right, (((0,), (0,)), ((), ())), preferred_element_type=jnp.float32
    )


def contract_cols(left, right):
    return lax.dot_general(
        left, right, (((1,), (1,)), ((), ())), preferred_element_type=jnp.float32
    )


def combine_pairs(earlier, later):
    s_max_a, s_sum_a, t_max_a, t_sum_a = earlier
    s_max_b, s_sum_b, t_max_b, t_sum_b = later
    s_max = jnp.maximum(s_max_a, s_max_b)
    t_max = jnp.maximum(t_max_a, t_max_b)
    s_sum = s_sum_a * jnp.exp(s_max_a - s_max) + s_sum_b * jnp.exp(s_max_b - s_max)
    t_sum = t_sum_a * jnp.exp(t_max_a - t_max) + t_sum_b * jnp.exp(t_max_b - t_max)
    return (s_max, s_sum, t_max, t_sum)


def per_device(hidden, embed_grad, token_ids, loss_weight, teacher_logits, head):
    vocab_width = head.shape[1]
    hidden_cols, embed_cols = (
        lax.all_to_all(hidden, "dp", split_axis=1, concat_axis=0, tiled=True),
        lax.all_to_all(embed_grad, "dp", split_axis=1, concat_axis=0, tiled=True),
    )
    student = lax.psum_scatter(
        jnp.dot(hidden_cols, head, preferred_element_type=jnp.float32),
        "dp",
        scatter_dimension=0,
        tiled=True,
    )
    teacher = teacher_logits.astype(jnp.float32)
    student_max = jnp.max(student, axis=1)
    teacher_max = jnp.max(teacher, axis=1)
    student_sum = jnp.sum(jnp.exp(student - student_max[:, None]), axis=1)
    teacher_sum = jnp.sum(jnp.exp(teacher - teacher_max[:, None]), axis=1)
    student_top, student_total, teacher_top, teacher_total = combined_all(
        (student_max, student_sum, teacher_max, teacher_sum), "vocab", combine_pairs
    )
    student_norm = student_top + jnp.log(student_total)
    teacher_norm = teacher_top + jnp.log(teacher_total)
    gap = (
        loss_weight[:, None]
        * (jnp.exp(student - student_norm[:, None]) - jnp.exp(teacher - teacher_norm[:, None]))
    ).astype(jnp.bfloat16)
    vocab_ids = lax.axis_index("vocab") * vocab_width + jnp.arange(vocab_width, dtype=jnp.int32)
    gap_piece = lax.all_gather(gap, "dp", axis=0, tiled=True)
    id_piece = lax.all_gather(token_ids, "dp", axis=0, tiled=True)
    lookup = (id_piece[:, None] == vocab_ids[None, :]).astype(jnp.bfloat16)
    grad_rows = contract_rows(hidden_cols, gap_piece) + contract_rows(embed_cols, lookup)
    back_cols = contract_cols(gap_piece, head)
    head_grad, back_cols = (grad_rows, back_cols)
    regrouped = lax.all_to_all(back_cols, "dp", split_axis=0, concat_axis=1, tiled=True)
    grad_hidden = lax.psum_scatter(regrouped, "vocab", scatter_dimension=1, tiled=True).astype(
        jnp.bfloat16
    )
    return (grad_hidden, head_grad)


def solution(mesh):
    placed = (P("dp", None), P("dp", None), P("dp"), P("dp"), P("dp", "vocab"), P("dp", "vocab"))
    return jax.shard_map(
        per_device,
        mesh=mesh,
        in_specs=placed,
        out_specs=(P("dp", "vocab"), P("dp", "vocab")),
        check_vma=False,
    )
```

profile of v0, /device:TPU:0, one launch (start us, length us, event | category | flops | bytes accessed | tf_op | source)
XLA Modules:
  0.0 173.7 jit_solution(2264943251010884728)
XLA Ops:
  7.2 0.0 reduce-scatter.3.cloned.1.call-start
  7.2 10.2 %all_to_all.57 = bf16[8,8,512]{2,0,1:T(8,128)(2,1)S(1)} all-to-all(bf16[8,8,512]{2,0,1:T(8,128)(2,1)} %bitcast.60), channel_id=1, replica_groups=mesh['dp'=8,'vocab'=4] {'dp'}, dimensions={1} | all-to-all | bytes 131072 | tf_op jit(solution)/shard_map/all_to_all | solution.py:43
  17.4 0.0 copy-start.1
  17.4 0.0 copy-start.6
  17.4 6.3 %fusion.22 = f32[64,8192]{1,0:T(8,128)} fusion(bf16[512,8192]{1,0:T(8,128)(2,1)} %param.13, bf16[8,8,512]{2,0,1:T(8,128)(2,1)S(1)} %all_to_all.57), kind=kOutput, calls=%fused_computation.31 | convolution fusion | flops 536870912 | bytes 10551296 | tf_op jit(solution)/shard_map/dot_general | solution.py:47
  23.8 0.0 reduce-scatter.3.cloned.1.call-update
  23.8 0.0 all-gather.6.cloned.1.call-start
  23.8 0.0 copy-done.1
  23.8 0.2 reduce_max.28
  24.0 0.0 copy-done.6
  24.0 0.6 dynamic-slice
  25.3 0.3 fusion.14
  25.6 0.2 dynamic-update-slice.3
  25.8 0.1 convert_dynamic-update-slice_fusion
  25.9 38.6 %reduce-scatter.3.cloned.1.call-done = f32[8,8192]{1,0:T(8,128)} async-done(((f32[64,8192]{1,0:T(8,128)}), f32[8,8192]{1,0:T(8,128)}) %reduce-scatter.3.cloned.1.call-update) | async-done | bytes 262160 | tf_op jit(solution)/shard_map/reduce_scatter | solution.py:46
  64.5 1.1 reduce_max.27
  65.6 0.2 dynamic-update-slice
  65.8 1.2 exponential_reduce_fusion
  67.0 0.2 dynamic-update-slice.1
  67.3 11.7 %all-reduce.5 = (f32[32]{0:T(128)S(1)}, f32[32]{0:T(128)S(1)}, f32[32]{0:T(128)S(1)}, f32[32]{0:T(128)S(1)}) all-reduce(f32[32]{0:T(128)S(1)} %dynamic-update-slice, f32[32]{0:T(128)S(1)} %dynamic-update-slice.1, f32[32]{0:T(128)S(1)} %convert_dynamic-update-slice_fusion, ...), channel_id=2, replica_groups=mesh['dp'=8,'vocab'=4] {'vocab'}, use_global_device_ids=true, to_apply=%add | all-reduce | flops 128 | bytes 1024
  78.9 0.1 reshape.35
  79.0 0.1 reshape.36
  79.1 0.1 reshape.37
  79.2 0.1 reshape.38
  79.3 0.1 while.21
  79.4 0.0 copy-done.3
  79.4 1.8 %fusion.18 = bf16[8,8192]{1,0:T(8,128)(2,1)} fusion(bf16[8,8192]{1,0:T(8,128)(2,1)S(1)} %copy-done.1, f32[8,8192]{1,0:T(8,128)} %reduce-scatter.3.cloned.1.call-done, f32[8]{0:T(128)S(1)} %get-tuple-element.259, f32[8]{0:T(128)S(1)} %get-tuple-element.260, f32[8]{0:T(128)S(1)} %copy-done.3), kind=kLoop, calls=%fused_computation.26 | loop fusion | flops 393216 | bytes 524384 | tf_op jit(solution)/shard_map/convert_element_type | solution.py:65
  81.2 0.0 all-gather.6.cloned.1.call-update
  81.2 20.8 %all-gather.6.cloned.1.call-done = bf16[64,8192]{1,0:T(8,128)(2,1)} async-done(((bf16[8,8192]{1,0:T(8,128)(2,1)}), bf16[64,8192]{1,0:T(8,128)(2,1)}) %all-gather.6.cloned.1.call-update) | async-done | bytes 1048592 | tf_op jit(solution)/shard_map/all_gather | solution.py:67
  102.0 7.1 %convolution_bitcast_fusion = f32[8,8,512]{2,1,0:T(8,128)} fusion(bf16[64,8192]{1,0:T(8,128)(2,1)} %all-gather.6.cloned.1.call-done, bf16[512,8192]{1,0:T(8,128)(2,1)} %param.13), kind=kOutput, calls=%fused_computation.16 | convolution fusion | flops 536870912 | bytes 9568256 | tf_op jit(solution)/shard_map/dot_general | solution.py:25
  109.1 3.4 %all-to-all-start.1 = ((f32[8,8,512]{2,1,0:T(8,128)}), f32[8,8,512]{2,1,0:T(8,128)S(1)}, u32[]{:S(2)}, u32[]{:S(2)}) async-start(f32[8,8,512]{2,1,0:T(8,128)} %convolution_bitcast_fusion), calls=%async_computation.2 | async-start | bytes 262144 | tf_op jit(solution)/shard_map/all_to_all | solution.py:73
  112.5 0.0 copy-done.5
  112.5 0.6 dynamic-slice.4
  113.7 0.0 copy-done.4
  113.7 0.2 dynamic-update-slice.4
  114.0 8.4 %all-reduce.4 = s32[64]{0:T(128)S(1)} all-reduce(s32[64]{0:T(128)S(1)} %dynamic-update-slice.4), channel_id=1, replica_groups=mesh['dp'=8,'vocab'=4] {'dp'}, use_global_device_ids=true, to_apply=%add.4 | all-reduce | flops 64 | bytes 512
  122.4 0.0 all-to-all-done.1
  122.4 0.0 copy-start.2
  122.4 3.4 %all-to-all-start.2 = ((bf16[8,8,512]{2,0,1:T(8,128)(2,1)}), bf16[8,8,512]{2,0,1:T(8,128)(2,1)S(1)}, u32[]{:S(2)}, u32[]{:S(2)}) async-start(bf16[8,8,512]{2,0,1:T(8,128)(2,1)} %bitcast.13), calls=%async_computation.4 | async-start | bytes 131072 | tf_op jit(solution)/shard_map/all_to_all | solution.py:44
  125.8 0.0 reduce-scatter.5.cloned.1.call-start
  125.8 0.0 copy-done
  125.8 8.5 %fusion.20 = f32[8192,512]{1,0:T(8,128)} fusion(bf16[64,8192]{1,0:T(8,128)(2,1)S(1)} %copy-done, bf16[8,8,512]{2,0,1:T(8,128)(2,1)S(1)} %all_to_all.57), kind=kOutput, calls=%fused_computation.29 | convolution fusion | flops 536870912 | bytes 17891328 | tf_op jit(solution)/shard_map/dot_general | solution.py:19
  134.4 0.0 copy-done.2
  134.4 0.0 reduce-scatter.5.cloned.1.call-update
  134.4 0.0 all-to-all-done.2
  134.4 13.9 %add_bitcast_fusion = f32[512,8192]{0,1:T(8,128)} fusion(f32[8192,512]{1,0:T(8,128)} %fusion.20, s32[8192]{0:T(1024)S(1)} %iota_add_fusion, s32[64]{0:T(128)S(1)} %all-reduce.4, bf16[8,8,512]{2,0,1:T(8,128)(2,1)S(1)} %all-to-all-done.2), kind=kOutput, calls=%fused_computation.14 | convolution fusion | flops 541589504 | bytes 33652992 | tf_op jit(solution)/shard_map/dot_general | solution.py:19
  148.4 17.4 %copy.8 = f32[512,8192]{1,0:T(8,128)} copy(f32[512,8192]{0,1:T(8,128)} %add_bitcast_fusion) | data formatting | bytes 33554432
  165.8 1.4 convert_element_type.12
  (16 shorter events, 0.1 us)
Async XLA Ops:
  7.2 57.3 %reduce-scatter.3.cloned.1.call-start = ((), (), s32[]{:S(2)}) async-start(), calls=%async_computation.5 | async-start | bytes 2359296 | tf_op jit(solution)/shard_map/reduce_scatter | solution.py:46
  17.4 6.4 %copy-start.1 = (bf16[8,8192]{1,0:T(8,128)(2,1)S(1)}, bf16[8,8192]{1,0:T(8,128)(2,1)}, u32[]{:S(2)}) copy-start(bf16[8,8192]{1,0:T(8,128)(2,1)} %param.12) | copy-start | bytes 393220
  17.4 6.6 %copy-start.6 = (u32[32]{0:T(128)S(1)}, u32[32]{0:T(128)}, u32[]{:S(2)}) copy-start(u32[32]{0:T(128)} %constant.69) | copy-start | bytes 388
  17.4 62.0 %copy-start.3 = (f32[8]{0:T(128)S(1)}, f32[8]{0:T(128)}, u32[]{:S(2)}) copy-start(f32[8]{0:T(128)} %param.11) | copy-start | bytes 100
  23.7 88.7 %copy-start.5 = (u32[32]{0:T(128)S(1)}, u32[32]{0:T(128)}, u32[]{:S(2)}) copy-start(u32[32]{0:T(128)} %constant.89) | copy-start | bytes 388
  23.7 90.0 %copy-start.4 = (s32[8]{0:T(128)S(1)}, s32[8]{0:T(128)}, u32[]{:S(2)}) copy-start(s32[8]{0:T(128)} %param.10) | copy-start | bytes 100
  23.8 78.2 %all-gather.6.cloned.1.call-start = ((), (), s32[]{:S(2)}) async-start(), calls=%async_computation.6 | async-start | bytes 1179648 | tf_op jit(solution)/shard_map/all_gather | solution.py:67
  102.0 23.9 %copy-start = (bf16[64,8192]{1,0:T(8,128)(2,1)S(1)}, bf16[64,8192]{1,0:T(8,128)(2,1)}, u32[]{:S(2)}) copy-start(bf16[64,8192]{1,0:T(8,128)(2,1)} %all-gather.6.cloned.1.call-done) | copy-start | bytes 3145732
  109.1 13.3 %all-to-all-start.1 = ((f32[8,8,512]{2,1,0:T(8,128)}), f32[8,8,512]{2,1,0:T(8,128)S(1)}, u32[]{:S(2)}, u32[]{:S(2)}) async-start(f32[8,8,512]{2,1,0:T(8,128)} %convolution_bitcast_fusion), calls=%async_computation.2 | async-start | bytes 262144 | tf_op jit(solution)/shard_map/all_to_all | solution.py:73
  122.4 12.0 %copy-start.2 = (f32[8,8,512]{2,1,0:T(8,128)}, f32[8,8,512]{2,1,0:T(8,128)S(1)}, u32[]{:S(2)}) copy-start(f32[8,8,512]{2,1,0:T(8,128)S(1)} %all-to-all-done.1) | copy-start | bytes 393220
  122.4 12.0 %all-to-all-start.2 = ((bf16[8,8,512]{2,0,1:T(8,128)(2,1)}), bf16[8,8,512]{2,0,1:T(8,128)(2,1)S(1)}, u32[]{:S(2)}, u32[]{:S(2)}) async-start(bf16[8,8,512]{2,0,1:T(8,128)(2,1)} %bitcast.13), calls=%async_computation.4 | async-start | bytes 131072 | tf_op jit(solution)/shard_map/all_to_all | solution.py:44
  125.8 40.0 %reduce-scatter.5.cloned.1.call-start = ((), (), s32[]{:S(2)}) async-start(), calls=%async_computation.7 | async-start | bytes 163840 | tf_op jit(solution)/shard_map/reduce_scatter | solution.py:74
Sparse Core Ops, SparseCore 0:
  23.9 40.5 reduce-scatter.2
  81.3 20.5 all-gather.5
  134.5 20.7 reduce-scatter.4
where the time goes:
time: 175 us; the launch traced here: 174 us
  waiting for transfers between devices  59.4 us (34%)
  matrix products  35.9 us (21%)
  blocking collectives  30.3 us (17%)
  local copies, waits for them, and re-layouts  20 us (11%)
  between operations  15.2 us (9%)
  starting transfers between devices  6.86 us (4%)
  other arithmetic  6.1 us (3%)
    reduce_scatter x1, waiting for transfers between devices, per_device(): lax.psum_scatter(jnp.dot(hidden_cols, head, preferred_element_type=jnp.fl...  38.6 us
    dot_general x2, matrix products, contract_rows(): lax.dot_general(left, right, (((0,), (0,)), ((), ())), preferred_element_...  22.5 us
    all_gather x1, waiting for transfers between devices, per_device(): gap_piece = lax.all_gather(gap, 'dp', axis=0, tiled=True)  20.8 us
    unnamed x2, blocking collectives  20.1 us
    unnamed x26, local copies, waits for them, and re-layouts  19.6 us
    all_to_all x1, blocking collectives, per_device(): lax.all_to_all(hidden, 'dp', split_axis=1, concat_axis=0, tiled=True)  10.2 us
    dot_general x1, matrix products, contract_cols(): lax.dot_general(left, right, (((1,), (1,)), ((), ())), preferred_element_...  7.1 us
    dot_general x1, matrix products, per_device(): jnp.dot(hidden_cols, head, preferred_element_type=jnp.float32)  6.31 us
  transfers between devices with their start and end apart: 5, of which 2 were waited for; matrix products, arithmetic and copies ran while one was open for 24% of the time, Pallas kernels for 0%

commit v1 on v0

--- a/solution.py
+++ b/solution.py
@@ -40,7 +40,10 @@
 def per_device(hidden, embed_grad, token_ids, loss_weight, teacher_logits, head):
     vocab_width = head.shape[1]
     hidden_cols, embed_cols = (
-        lax.all_to_all(hidden, "dp", split_axis=1, concat_axis=0, tiled=True),
+        jnp.concatenate(
+            lax.all_to_all(jnp.stack(jnp.split(hidden, lax.axis_size("dp"), axis=1)), "dp", 0, 0),
+            axis=0,
+        ),
         lax.all_to_all(embed_grad, "dp", split_axis=1, concat_axis=0, tiled=True),
     )
     student = lax.psum_scatter(

time: 175 us -> 157 us (0.90)
  local copies, waits for them, and re-layouts: 20 us -> 8.75 us
  waiting for transfers between devices: 59.4 us -> 52.7 us
    all_gather x1, waiting for transfers between devices: 20.8 us -> 7.45 us  [per_device(): gap_piece = lax.all_gather(gap, 'dp', axis=0, tiled=True)]
    unnamed x26 -> x32, local copies, waits for them, and re-layouts: 19.6 us -> 7.72 us
    reduce_scatter x1, waiting for transfers between devices: 0.01 us -> 6.6 us  [per_device(): lax.psum_scatter(regrouped, 'vocab', scatter_dimension=1, tiled=True)]
  transfers between devices with their start and end apart: 5 -> 5, of which waited for: 2 -> 3; matrix products, arithmetic and copies ran while one was open for 24% -> 21% of each run, Pallas kernels for 0% -> 0%
where the time goes in v1:
time: 157 us; the launch traced here: 156 us
  waiting for transfers between devices  52.7 us (34%)
  matrix products  36.2 us (23%)
  blocking collectives  30.1 us (19%)
  between operations  15.2 us (10%)
  local copies, waits for them, and re-layouts  8.75 us (6%)
  starting transfers between devices  6.86 us (4%)
  other arithmetic  6.1 us (4%)
    reduce_scatter x1, waiting for transfers between devices, per_device(): lax.psum_scatter(jnp.dot(hidden_cols, head, preferred_element_type=jnp.fl...  38.6 us
    dot_general x2, matrix products, contract_rows(): lax.dot_general(left, right, (((0,), (0,)), ((), ())), preferred_element_...  22.9 us
    unnamed x2, blocking collectives  20.1 us
    all_to_all x1, blocking collectives, per_device(): lax.all_to_all(jnp.stack(jnp.split(hidden, lax.axis_size('dp'), axis=1)),...  10 us
    unnamed x32, local copies, waits for them, and re-layouts  7.72 us
    all_gather x1, waiting for transfers between devices, per_device(): gap_piece = lax.all_gather(gap, 'dp', axis=0, tiled=True)  7.45 us
    dot_general x1, matrix products, contract_cols(): lax.dot_general(left, right, (((1,), (1,)), ((), ())), preferred_element_...  7.03 us
    reduce_scatter x1, waiting for transfers between devices, per_device(): lax.psum_scatter(regrouped, 'vocab', scatter_dimension=1, tiled=True)  6.6 us
  transfers between devices with their start and end apart: 5, of which 3 were waited for; matrix products, arithmetic and copies ran while one was open for 21% of the time, Pallas kernels for 0%

profile of v1, /device:TPU:0, one launch (start us, length us, event | category | flops | bytes accessed | tf_op | source)
XLA Modules:
  0.0 155.9 jit_solution(14438258762942651453)
XLA Ops:
  7.2 0.0 reduce-scatter.3.cloned.1.call-start
  7.2 0.7 constant_dynamic-update-slice_fusion.7
  7.9 0.7 constant_dynamic-update-slice_fusion.6
  8.6 0.7 constant_dynamic-update-slice_fusion.5
  9.3 0.7 constant_dynamic-update-slice_fusion.4
  10.0 0.7 constant_dynamic-update-slice_fusion.3
  10.7 0.7 constant_dynamic-update-slice_fusion.2
  11.4 0.7 constant_dynamic-update-slice_fusion.1
  12.1 0.7 constant_dynamic-update-slice_fusion
  12.8 10.0 %all_to_all.43 = bf16[8,8,512]{2,1,0:T(8,128)(2,1)S(1)} all-to-all(bf16[8,8,512]{2,1,0:T(8,128)(2,1)S(1)} %constant_dynamic-update-slice_fusion), channel_id=1, replica_groups=mesh['dp'=8,'vocab'=4] {'dp'}, dimensions={0} | all-to-all | bytes 131072 | tf_op jit(solution)/shard_map/all_to_all | solution.py:44
  22.8 0.0 copy-start.4
  22.8 6.3 %fusion.22 = f32[64,8192]{1,0:T(8,128)} fusion(bf16[512,8192]{1,0:T(8,128)(2,1)} %param.13, bf16[8,8,512]{2,1,0:T(8,128)(2,1)S(1)} %all_to_all.43), kind=kOutput, calls=%fused_computation.31 | convolution fusion | flops 536870912 | bytes 10551296 | tf_op jit(solution)/shard_map/dot_general | solution.py:50
  29.1 0.0 reduce-scatter.3.cloned.1.call-update
  29.2 0.0 all-gather.6.cloned.1.call-start
  29.2 0.2 reduce_max.28
  29.4 0.6 dynamic-slice
  30.7 0.3 fusion.15
  30.9 0.2 dynamic-update-slice.3
  31.2 0.1 convert_dynamic-update-slice_fusion
  31.3 38.6 %reduce-scatter.3.cloned.1.call-done = f32[8,8192]{1,0:T(8,128)} async-done(((f32[64,8192]{1,0:T(8,128)}), f32[8,8192]{1,0:T(8,128)}) %reduce-scatter.3.cloned.1.call-update) | async-done | bytes 262160 | tf_op jit(solution)/shard_map/reduce_scatter | solution.py:49
  69.8 1.1 reduce_max.27
  71.0 0.2 dynamic-update-slice
  71.2 1.2 exponential_reduce_fusion
  72.4 0.2 dynamic-update-slice.1
  72.7 11.7 %all-reduce.5 = (f32[32]{0:T(128)S(1)}, f32[32]{0:T(128)S(1)}, f32[32]{0:T(128)S(1)}, f32[32]{0:T(128)S(1)}) all-reduce(f32[32]{0:T(128)S(1)} %dynamic-update-slice, f32[32]{0:T(128)S(1)} %dynamic-update-slice.1, f32[32]{0:T(128)S(1)} %convert_dynamic-update-slice_fusion, ...), channel_id=2, replica_groups=mesh['dp'=8,'vocab'=4] {'vocab'}, use_global_device_ids=true, to_apply=%add | all-reduce | flops 128 | bytes 1024
  84.3 0.1 reshape.36
  84.4 0.1 reshape.37
  84.5 0.1 reshape.38
  84.6 0.1 reshape.39
  84.7 0.1 while.21
  84.8 1.8 %fusion.19 = bf16[8,8192]{1,0:T(8,128)(2,1)} fusion(bf16[8,8192]{1,0:T(8,128)(2,1)S(1)} %copy-done.1, f32[8,8192]{1,0:T(8,128)} %reduce-scatter.3.cloned.1.call-done, f32[8]{0:T(128)S(1)} %get-tuple-element.257, f32[8]{0:T(128)S(1)} %get-tuple-element.258, f32[8]{0:T(128)S(1)} %copy-done.3), kind=kLoop, calls=%fused_computation.27 | loop fusion | flops 393216 | bytes 524384 | tf_op jit(solution)/shard_map/convert_element_type | solution.py:68
  86.6 0.0 all-gather.6.cloned.1.call-update
  86.6 3.4 %all-to-all-start.2 = ((bf16[8,8,512]{2,0,1:T(8,128)(2,1)}), bf16[8,8,512]{2,0,1:T(8,128)(2,1)S(1)}, u32[]{:S(2)}, u32[]{:S(2)}) async-start(bf16[8,8,512]{2,0,1:T(8,128)(2,1)} %bitcast.18), calls=%async_computation.4 | async-start | bytes 131072 | tf_op jit(solution)/shard_map/all_to_all | solution.py:47
  90.0 0.6 dynamic-slice.4
  91.2 0.2 dynamic-update-slice.4
  91.5 8.4 %all-reduce.4 = s32[64]{0:T(128)S(1)} all-reduce(s32[64]{0:T(128)S(1)} %dynamic-update-slice.4), channel_id=1, replica_groups=mesh['dp'=8,'vocab'=4] {'dp'}, use_global_device_ids=true, to_apply=%add.4 | all-reduce | flops 64 | bytes 512
  99.9 7.5 %all-gather.6.cloned.1.call-done = bf16[64,8192]{1,0:T(8,128)(2,1)} async-done(((bf16[8,8192]{1,0:T(8,128)(2,1)}), bf16[64,8192]{1,0:T(8,128)(2,1)}) %all-gather.6.cloned.1.call-update) | async-done | bytes 1048592 | tf_op jit(solution)/shard_map/all_gather | solution.py:70
  107.4 7.0 %convolution_bitcast_fusion = f32[8,8,512]{2,1,0:T(8,128)} fusion(bf16[64,8192]{1,0:T(8,128)(2,1)} %all-gather.6.cloned.1.call-done, bf16[512,8192]{1,0:T(8,128)(2,1)} %param.13), kind=kOutput, calls=%fused_computation.17 | convolution fusion | flops 536870912 | bytes 9568256 | tf_op jit(solution)/shard_map/dot_general | solution.py:25
  114.4 0.0 all-to-all-done.2
  114.4 3.4 %all-to-all-start.1 = ((f32[8,8,512]{2,1,0:T(8,128)}), f32[8,8,512]{2,1,0:T(8,128)S(1)}, u32[]{:S(2)}, u32[]{:S(2)}) async-start(f32[8,8,512]{2,1,0:T(8,128)} %convolution_bitcast_fusion), calls=%async_computation.2 | async-start | bytes 262144 | tf_op jit(solution)/shard_map/all_to_all | solution.py:76
  117.8 0.0 reduce-scatter.5.cloned.1.call-start
  117.8 8.6 %fusion.10 = f32[8192,512]{0,1:T(8,128)} fusion(s32[8192]{0:T(1024)S(1)} %iota_add_fusion, s32[64]{0:T(128)S(1)} %all-reduce.4, bf16[8,8,512]{2,0,1:T(8,128)(2,1)S(1)} %all-to-all-done.2), kind=kOutput, calls=%fused_computation.15 | convolution fusion | flops 537395200 | bytes 16875776 | tf_op jit(solution)/shard_map/dot_general | solution.py:19
  126.4 0.0 all-to-all-done.1
  126.4 0.7 copy-done.2
  127.0 0.0 reduce-scatter.5.cloned.1.call-update
  127.1 14.3 %bitcast_add_fusion = f32[512,8192]{1,0:T(8,128)} fusion(f32[8192,512]{0,1:T(8,128)} %fusion.10, bf16[64,8192]{1,0:T(8,128)(2,1)S(1)} %copy-done, bf16[8,8,512]{2,1,0:T(8,128)(2,1)S(1)} %all_to_all.43), kind=kOutput, calls=%fused_computation.14 | convolution fusion | flops 541065216 | bytes 34668544 | tf_op jit(solution)/shard_map/dot_general | solution.py:19
  141.4 6.6 %reduce-scatter.5.cloned.1.call-done = f32[8,1024]{1,0:T(8,128)} async-done(((f32[8,4096]{1,0:T(8,128)}), f32[8,1024]{1,0:T(8,128)}) %reduce-scatter.5.cloned.1.call-update) | async-done | bytes 32784 | tf_op jit(solution)/shard_map/reduce_scatter | solution.py:77
  148.0 1.4 convert_element_type.12
  (23 shorter events, 0.1 us)
Async XLA Ops:
  7.2 62.7 %reduce-scatter.3.cloned.1.call-start = ((), (), s32[]{:S(2)}) async-start(), calls=%async_computation.5 | async-start | bytes 2359296 | tf_op jit(solution)/shard_map/reduce_scatter | solution.py:49
  22.8 6.4 %copy-start.1 = (bf16[8,8192]{1,0:T(8,128)(2,1)S(1)}, bf16[8,8192]{1,0:T(8,128)(2,1)}, u32[]{:S(2)}) copy-start(bf16[8,8192]{1,0:T(8,128)(2,1)} %param.12) | copy-start | bytes 393220
  22.8 6.6 %copy-start.6 = (u32[32]{0:T(128)S(1)}, u32[32]{0:T(128)}, u32[]{:S(2)}) copy-start(u32[32]{0:T(128)} %constant.69) | copy-start | bytes 388
  22.8 62.0 %copy-start.3 = (f32[8]{0:T(128)S(1)}, f32[8]{0:T(128)}, u32[]{:S(2)}) copy-start(f32[8]{0:T(128)} %param.11) | copy-start | bytes 100
  22.8 67.2 %copy-start.5 = (u32[32]{0:T(128)S(1)}, u32[32]{0:T(128)}, u32[]{:S(2)}) copy-start(u32[32]{0:T(128)} %constant.89) | copy-start | bytes 388
  22.8 68.4 %copy-start.4 = (s32[8]{0:T(128)S(1)}, s32[8]{0:T(128)}, u32[]{:S(2)}) copy-start(s32[8]{0:T(128)} %param.10) | copy-start | bytes 100
  29.2 78.2 %all-gather.6.cloned.1.call-start = ((), (), s32[]{:S(2)}) async-start(), calls=%async_computation.6 | async-start | bytes 1179648 | tf_op jit(solution)/shard_map/all_gather | solution.py:70
  86.6 27.8 %all-to-all-start.2 = ((bf16[8,8,512]{2,0,1:T(8,128)(2,1)}), bf16[8,8,512]{2,0,1:T(8,128)(2,1)S(1)}, u32[]{:S(2)}, u32[]{:S(2)}) async-start(bf16[8,8,512]{2,0,1:T(8,128)(2,1)} %bitcast.18), calls=%async_computation.4 | async-start | bytes 131072 | tf_op jit(solution)/shard_map/all_to_all | solution.py:47
  114.4 12.0 %all-to-all-start.1 = ((f32[8,8,512]{2,1,0:T(8,128)}), f32[8,8,512]{2,1,0:T(8,128)S(1)}, u32[]{:S(2)}, u32[]{:S(2)}) async-start(f32[8,8,512]{2,1,0:T(8,128)} %convolution_bitcast_fusion), calls=%async_computation.2 | async-start | bytes 262144 | tf_op jit(solution)/shard_map/all_to_all | solution.py:76
  117.8 9.3 %copy-start = (bf16[64,8192]{1,0:T(8,128)(2,1)S(1)}, bf16[64,8192]{1,0:T(8,128)(2,1)}, u32[]{:S(2)}) copy-start(bf16[64,8192]{1,0:T(8,128)(2,1)} %all-gather.6.cloned.1.call-done) | copy-start | bytes 3145732
  117.8 30.2 %reduce-scatter.5.cloned.1.call-start = ((), (), s32[]{:S(2)}) async-start(), calls=%async_computation.7 | async-start | bytes 163840 | tf_op jit(solution)/shard_map/reduce_scatter | solution.py:77
  126.4 0.7 copy-start.2
Sparse Core Ops, SparseCore 0:
  29.3 40.5 reduce-scatter.2
  86.7 20.5 all-gather.5
  127.2 20.7 reduce-scatter.4
